TPU v7x, 32 devices: a whole 2x2x4 slice. The times are simulated.
32 devices in a mesh: dp: 4 (over x, core), tensor: 8 (over z, y).
Axes of the slice: x: 2, y: 2, z: 4, core: 2. Of those that a mesh axis runs over, the one named last changes fastest.
Arguments:
- tokens: bfloat16 [96, 8, 4096], P('dp'), may hold values from -6 to 6
- norm_gain: float32 [4096], replicated, may hold values from 0.1 to 1.9
- in_weight: bfloat16 [4096, 2, 4096], P(None, None, 'tensor'), may hold values from -0.09375 to 0.09375
- group_weight: bfloat16 [4096, 1024], P(None, 'tensor'), may hold values from -0.09375 to 0.09375
- step_weight: bfloat16 [4096, 64], P(None, 'tensor'), may hold values from -0.09375 to 0.09375
- value_kernel: bfloat16 [4, 4096], P(None, 'tensor'), may hold values from -3 to 3
- value_offset: bfloat16 [4096], P('tensor'), may hold values from -3 to 3
- group_kernel: bfloat16 [4, 1024], P(None, 'tensor'), may hold values from -3 to 3
- group_offset: bfloat16 [1024], P('tensor'), may hold values from -3 to 3
- step_bias: float32 [64], P('tensor'), may hold values from -4 to 1
- decay_rate: float32 [64], P('tensor'), may hold values from 0.05 to 2
- skip_gain: float32 [64], P('tensor'), may hold values from 0.5 to 2
- out_gain: float32 [4096], P('tensor'), may hold values from 0.1 to 1.9
- out_weight: bfloat16 [4096, 4096], P('tensor'), may hold values from -0.09375 to 0.09375
- scan_state: bfloat16 [96, 64, 64, 128], P('dp', 'tensor'), may hold values from -6 to 6
- value_cache: bfloat16 [96, 3, 4096], P('dp', None, 'tensor'), may hold values from -6 to 6
- group_cache: bfloat16 [96, 3, 1024], P('dp', None, 'tensor'), may hold values from -6 to 6
- accepted: int32 [96], P('dp'), may hold values from 0 to 8, as said below
- draft_lengths: int32 [96], P('dp'), may hold values from 1 to 8, as said below
- live_flags: int32 [96], P('dp'), may hold values 0 or 1
Outputs:
- layer_out: bfloat16 [96, 8, 4096], P('dp')
- kept_state: bfloat16 [96, 64, 64, 128], P('dp', 'tensor')
- value_kept: bfloat16 [96, 3, 4096], P('dp', None, 'tensor')
- group_kept: bfloat16 [96, 3, 1024], P('dp', None, 'tensor')
- accepted_total: int32 [1], replicated
Inputs may be any that keep to these rules, and one draw needn't show every extreme that they name: `draft_lengths`: positions at or after a request's draft length are padding. `accepted`: never more than the same request's draft length.
All inputs are finite; a program needn't handle non-finite values.
Results may differ from a plain program's by a relative error of at most 0.012.
Values may be sent and summed in bfloat16 or wider, within the bound.
A program may use at most 128 MiB of HBM per device.

v0:
```python
import jax
import jax.numpy as jnp
from jax import lax
from jax.sharding import PartitionSpec as P

EPSILON = 1e-05
HIGHEST_PRECISION = lax.Precision.HIGHEST


def swapped(value, axis, distance):
    mask = 2**distance
    pairs = [(source, source ^ mask) for source in range(lax.axis_size(axis))]
    return lax.ppermute(value, axis, pairs)


def convolve(window, fresh_rows, kernel, offset):
    sequence = jnp.concatenate([window, fresh_rows], axis=1)
    length = fresh_rows.shape[1]
    summed = jnp.zeros(fresh_rows.shape, jnp.float32) + offset.astype(jnp.float32)
    for tap_index in range(kernel.shape[0]):
        summed = summed + kernel[tap_index].astype(jnp.float32) * sequence[
            :, tap_index : tap_index + length
        ].astype(jnp.float32)
    return (jax.nn.silu(summed), sequence)


def keep_window(sequence, kept_count, width_rows):
    return jax.vmap(
        lambda single, start_row: lax.dynamic_slice_in_dim(single, start_row, width_rows, 0)
    )(sequence, kept_count)


def local(
    tokens,
    norm_gain,
    in_weight,
    group_weight,
    step_weight,
    value_kernel,
    value_offset,
    group_kernel,
    group_offset,
    step_bias,
    decay_rate,
    skip_gain,
    out_gain,
    out_weight,
    scan_state,
    value_cache,
    group_cache,
    accepted,
    draft_lengths,
    live_flags,
):
    requests, positions, model_width = tokens.shape
    row_total = requests * positions
    head_count = step_bias.shape[0]
    inner_dev = value_offset.shape[0]
    head_dim = inner_dev // head_count
    tap_count = value_kernel.shape[0]
    kept_count = accepted * live_flags
    accepted_total = lax.psum(jnp.sum(kept_count), "dp").reshape(1)
    flat_rows = tokens.reshape(row_total, model_width).astype(jnp.float32)
    normed = (
        flat_rows
        * lax.rsqrt(jnp.mean(flat_rows * flat_rows, axis=1, keepdims=True) + EPSILON)
        * norm_gain
    ).astype(jnp.bfloat16)
    parity = lax.axis_index("tensor") % 2
    in_flat = in_weight.reshape(in_weight.shape[0], 2 * inner_dev)
    inner_sum = jnp.dot(normed, in_flat, preferred_element_type=jnp.float32)
    group_sum = jnp.dot(normed, group_weight, preferred_element_type=jnp.float32)
    step_raw = jnp.dot(normed, step_weight, preferred_element_type=jnp.float32)
    inner_proj = inner_sum.astype(jnp.bfloat16).reshape(requests, positions, 2 * inner_dev)
    gate_part = inner_proj[:, :, :inner_dev]
    value_part = inner_proj[:, :, inner_dev:]
    group_proj = group_sum.astype(jnp.bfloat16).reshape(requests, positions, group_weight.shape[1])
    value_conv, value_seq = convolve(value_cache, value_part, value_kernel, value_offset)
    own_conv, group_seq = convolve(group_cache, group_proj, group_kernel, group_offset)
    other_conv = swapped(own_conv, "tensor", 0)
    input_map = jnp.where(parity == 0, own_conv, other_conv)
    output_map = jnp.where(parity == 0, other_conv, own_conv)
    values = value_conv.reshape(requests, positions, head_count, head_dim)
    step_size = jax.nn.softplus(step_raw.reshape(requests, positions, head_count) + step_bias)
    log_decay = -step_size * decay_rate
    prefix = jnp.concatenate(
        [jnp.zeros((requests, 1, head_count), jnp.float32), jnp.cumsum(log_decay, axis=1)], axis=1
    )
    after_step = prefix[:, 1:]
    alignment = jnp.einsum("rsn,rjn->rsj", output_map, input_map, precision=HIGHEST_PRECISION)
    causal = (jnp.arange(positions)[:, None] >= jnp.arange(positions)[None, :])[None, :, :, None]
    spread = after_step[:, :, None, :] - after_step[:, None, :, :]
    weights_mix = (
        jnp.where(causal, jnp.exp(jnp.where(causal, spread, 0.0)), 0.0)
        * step_size[:, None, :, :]
        * alignment[:, :, :, None]
    )
    within = jnp.einsum("rsjh,rjhp->rshp", weights_mix, values, precision=HIGHEST_PRECISION)
    initial = scan_state.astype(jnp.float32)
    carried = (
        jnp.einsum("rhpn,rsn->rshp", initial, output_map, precision=HIGHEST_PRECISION)
        * jnp.exp(after_step)[:, :, :, None]
    )
    head_out = within + carried + skip_gain[:, None] * values
    one_hot = (jnp.arange(positions + 1)[None, :] == kept_count[:, None]).astype(jnp.float32)
    prefix_kept = jnp.sum(one_hot[:, :, None] * prefix, axis=1)
    before_kept = (jnp.arange(positions)[None, :] < kept_count[:, None])[:, :, None]
    keep_weight = (
        jnp.where(
            before_kept,
            jnp.exp(jnp.where(before_kept, prefix_kept[:, None, :] - after_step, 0.0)),
            0.0,
        )
        * step_size
    )
    weighted = keep_weight[:, :, :, None] * values
    kept_state = (
        jnp.exp(prefix_kept)[:, :, None, None] * initial
        + jnp.einsum("rjhp,rjn->rhpn", weighted, input_map, precision=HIGHEST_PRECISION)
    ).astype(jnp.bfloat16)
    gated = head_out.reshape(row_total, inner_dev) * jax.nn.silu(
        gate_part.reshape(row_total, inner_dev).astype(jnp.float32)
    )
    own_squares = jnp.sum(gated * gated, axis=1)
    other_squares = swapped(own_squares, "tensor", 0)
    scale_rows = lax.rsqrt((own_squares + other_squares) / (2 * inner_dev) + EPSILON)
    valid_rows = (jnp.arange(positions)[None, :] < draft_lengths[:, None]) & (
        live_flags[:, None] == 1
    )
    normalized = jnp.where(
        valid_rows.reshape(row_total, 1), gated * scale_rows[:, None] * out_gain, 0.0
    ).astype(jnp.bfloat16)
    own_rows = lax.psum_scatter(
        jnp.dot(normalized, out_weight, preferred_element_type=jnp.float32),
        "tensor",
        scatter_dimension=0,
        tiled=True,
    ).astype(jnp.bfloat16)
    layer_rows = lax.all_gather(own_rows, "tensor", axis=0, tiled=True)
    value_kept = keep_window(value_seq, kept_count, tap_count - 1)
    group_kept = keep_window(group_seq, kept_count, tap_count - 1)
    return (
        layer_rows.reshape(requests, positions, model_width),
        kept_state,
        value_kept,
        group_kept,
        accepted_total,
    )


def solution(mesh):
    placed = (
        P("dp", None, None),
        P(),
        P(None, None, "tensor"),
        P(None, "tensor"),
        P(None, "tensor"),
        P(None, "tensor"),
        P("tensor"),
        P(None, "tensor"),
        P("tensor"),
        P("tensor"),
        P("tensor"),
        P("tensor"),
        P("tensor"),
        P("tensor", None),
        P("dp", "tensor", None, None),
        P("dp", None, "tensor"),
        P("dp", None, "tensor"),
        P("dp"),
        P("dp"),
        P("dp"),
    )
    return jax.shard_map(
        local,
        mesh=mesh,
        in_specs=placed,
        out_specs=(
            P("dp", None, None),
            P("dp", "tensor", None, None),
            P("dp", None, "tensor"),
            P("dp", None, "tensor"),
            P(),
        ),
        check_vma=False,
    )
```

profile of v0, /device:TPU:0, one launch (start us, length us, event | category | flops | bytes accessed | tf_op | source)
XLA Modules:
  0.0 192.2 jit_solution(2223818223673375586)
XLA Ops:
  7.2 1.9 fusion
  9.1 0.7 constant_dynamic-update-slice_fusion.1
  9.9 0.8 bitcast_convert_fusion.3
  11.4 2.1 %fusion.29 = bf16[24,8,128]{2,1,0:T(8,128)(2,1)S(1)} fusion(bf16[4096,128]{1,0:T(8,128)(2,1)S(1)} %copy-done, bf16[24,8,4096]{2,1,0:T(8,128)(2,1)} %param.20, f32[4096]{0:T(1024)} %param.21, f32[192]{0:T(256)S(1)} %rsqrt.16), kind=kOutput, calls=%fused_computation.26 | convolution fusion | flops 204496896 | bytes 2687744 | tf_op jit(solution)/shard_map/dot_general | solution.py:72
  13.6 3.1 %collective-permute-start = (f32[24,8,128]{2,0,1:T(8,128)S(1)}, f32[24,8,128]{2,0,1:T(8,128)}, u32[]{:S(2)}, u32[]{:S(2)}) collective-permute-start(f32[24,8,128]{2,0,1:T(8,128)S(1)} %divide_multiply_fusion.1), channel_id=1, source_target_pairs={{0,1},{1,0},{2,3},{3,2},{4,5},{5,4},{6,7},{7,6},{8,9},{9,8},{10,11... | collective-permute-start | bytes 294920 | tf_op jit(solution)/shard_map/ppermute | solution.py:13
  18.0 9.4 %copy.54 = bf16[512,8,2,512]{3,1,2,0:T(8,128)(2,1)} copy(bf16[512,8,2,512]{3,2,1,0:T(2,128)(2,1)} %bitcast.97) | data formatting | bytes 16777216
  27.4 5.3 %fusion.17 = bf16[24,8,1024]{2,1,0:T(8,128)(2,1)S(1)} fusion(bf16[4096,1024]{1,0:T(8,128)(2,1)} %bitcast.98, bf16[24,8,4096]{2,1,0:T(8,128)(2,1)S(1)} %copy-done.1, f32[4096]{0:T(1024)S(1)} %copy-done.12, f32[24,8]{1,0:T(8,128)S(1)} %add_rsqrt_fusion), kind=kOutput, calls=%fused_computation.22 | convolution fusion | flops 1613955072 | bytes 10371840 | tf_op jit(solution)/shard_map/dot_general | solution.py:71
  32.8 1.1 reshape.253
  34.7 2.1 %negate_multiply_fusion = (f32[24,8,8]{2,1,0:T(8,128)S(1)}, f32[24,8,8]{2,1,0:T(8,128)S(1)}) fusion(f32[8]{0:T(128)S(1)} %copy-done.13, f32[8]{0:T(128)S(1)} %copy-done.14, bf16[4096,8]{0,1:T(8,128)(2,1)S(1)} %copy-done.11, bf16[24,8,4096]{2,1,0:T(8,128)(2,1)} %param.20, f32[4096]{0:T(1024)S(1)} %copy-done.12, f32[24,8]{1,0:T(8,128)S(1)} %add_rsqrt_fusion), kind=kOutput, calls=%fused_computation.67 | convolution fusion | flops 15742464 | bytes 1667904 | tf_op jit(solution)/shard_map/dot_general | solution.py:73
  37.4 0.9 broadcast_select_fusion.1
  38.6 1.6 convolution_bitcast_fusion
  40.3 10.6 %multiply_reduce_fusion = (f32[24,8]{1,0:T(8,128)S(1)}, f32[24,8,8,64]{3,1,2,0:T(8,128)}) fusion(f32[24,8,8,64]{3,2,1,0:T(8,128)} %reshape.253, f32[24,8,8,64]{3,2,1,0:T(8,128)S(1)} %reshape.238, f32[8]{0:T(128)} %param.31, f32[24,8,8,64]{3,1,2,0:T(8,128)S(1)} %convolution_bitcast_fusion, f32[24,8,8]{1,2,0:T(8,128)S(1)} %copy.44, ...), kind=kOutput, calls=%fused_computation.28 | convolution fusion | flops 152076096 | bytes 4823840 | tf_op jit(solution)/shard_map/rhpn,rsn->rshp/dot_general | solution.py:101
  52.4 1.3 copy.46
  53.6 1.0 reshape.240
  54.6 0.9 collective-permute-done.1
  56.1 5.1 %fusion.52 = f32[192,4096]{1,0:T(8,128)} fusion(bf16[512,4096]{1,0:T(8,128)(2,1)} %param.33, f32[192,512]{1,0:T(8,128)} %reshape.240, f32[512]{0:T(512)} %param.32, f32[192]{0:T(256)S(1)} %add_rsqrt_fusion.1, pred[192]{0:T(512)(128)(4,1)} %and.23, bf16[24,8,1024]{2,1,0:T(8,128)(2,1)S(1)} %fusion.17), kind=kOutput, calls=%fused_computation.54 | convolution fusion | flops 806289408 | bytes 7933120 | tf_op jit(solution)/shard_map/dot_general | solution.py:134
  61.3 75.3 %reduce-scatter.2.cloned.1.call-done = f32[24,4096]{1,0:T(8,128)} async-done(((f32[192,4096]{1,0:T(8,128)}), f32[24,4096]{1,0:T(8,128)}) %reduce-scatter.2.cloned.1.call-update) | async-done | bytes 393232 | tf_op jit(solution)/shard_map/reduce_scatter | solution.py:133
  136.6 1.7 convert_element_type.206
  138.3 5.5 %psum.7 = s32[1]{0:T(128)} all-reduce(s32[1]{0:T(128)} %bitcast.22), channel_id=1, replica_groups=mesh['dp'=4,'tensor'=8] {'dp'}, use_global_device_ids=true, to_apply=%region_6.7 | all-reduce | flops 1 | bytes 8 | tf_op jit(solution)/shard_map/psum | solution.py:62
  143.9 1.6 gather_fusion
  145.5 1.4 gather_fusion.1
  147.2 13.1 %add_convert_fusion = bf16[24,8,64,128]{3,2,1,0:T(8,128)(2,1)} fusion(bf16[24,8,64,128]{3,2,1,0:T(8,128)(2,1)} %param.34, f32[24,8]{1,0:T(8,128)S(1)} %exp.46, f32[24,8,8,64]{3,2,1,0:T(8,128)S(1)} %broadcast_multiply_fusion, f32[24,8,128]{2,0,1:T(8,128)S(1)} %get-tuple-element.10), kind=kOutput, calls=%fused_computation.2 | convolution fusion | flops 157286400 | bytes 6783744 | tf_op jit(solution)/shard_map/rjhp,rjn->rhpn/dot_general | solution.py:119
  160.3 22.4 %all-gather.2.cloned.1.call-done = bf16[192,4096]{1,0:T(8,128)(2,1)} async-done(((bf16[24,4096]{1,0:T(8,128)(2,1)}), bf16[192,4096]{1,0:T(8,128)(2,1)}) %all-gather.2.cloned.1.call-update) | async-done | bytes 1572880 | tf_op jit(solution)/shard_map/all_gather | solution.py:139
  182.7 2.7 %copy.82 = bf16[24,8,4096]{2,1,0:T(8,128)(2,1)} copy(bf16[24,8,4096]{2,1,0:T(8,128)(2,1)} %bitcast.99) | data formatting | bytes 3145728
  (68 shorter events, 6.3 us)
Async XLA Ops:
  7.2 4.3 %copy-start = (bf16[4096,128]{1,0:T(8,128)(2,1)S(1)}, bf16[4096,128]{1,0:T(8,128)(2,1)}, u32[]{:S(2)}) copy-start(bf16[4096,128]{1,0:T(8,128)(2,1)} %param.23) | copy-start | bytes 3145732
  7.2 9.5 %copy-start.7 = (s32[24]{0:T(128)S(1)}, s32[24]{0:T(128)}, u32[]{:S(2)}) copy-start(s32[24]{0:T(128)} %param.37) | copy-start | bytes 292
  7.2 9.5 %copy-start.8 = (s32[24]{0:T(128)S(1)}, s32[24]{0:T(128)}, u32[]{:S(2)}) copy-start(s32[24]{0:T(128)} %param.39) | copy-start | bytes 292
  7.2 129.4 %reduce-scatter.2.cloned.1.call-start = ((), (), s32[]{:S(2)}) async-start(), calls=%async_computation.1 | async-start | bytes 3538944 | tf_op jit(solution)/shard_map/reduce_scatter | solution.py:133
  13.6 23.8 %collective-permute-start = (f32[24,8,128]{2,0,1:T(8,128)S(1)}, f32[24,8,128]{2,0,1:T(8,128)}, u32[]{:S(2)}, u32[]{:S(2)}) collective-permute-start(f32[24,8,128]{2,0,1:T(8,128)S(1)} %divide_multiply_fusion.1), channel_id=1, source_target_pairs={{0,1},{1,0},{2,3},{3,2},{4,5},{5,4},{6,7},{7,6},{8,9},{9,8},{10,11... | collective-permute-start | bytes 294920 | tf_op jit(solution)/shard_map/ppermute | solution.py:13
  18.0 9.4 %copy-start.1 = (bf16[24,8,4096]{2,1,0:T(8,128)(2,1)S(1)}, bf16[24,8,4096]{2,1,0:T(8,128)(2,1)}, u32[]{:S(2)}) copy-start(bf16[24,8,4096]{2,1,0:T(8,128)(2,1)} %param.20) | copy-start | bytes 4718596
  18.0 9.4 %copy-start.12 = (f32[4096]{0:T(1024)S(1)}, f32[4096]{0:T(1024)}, u32[]{:S(2)}) copy-start(f32[4096]{0:T(1024)} %param.21) | copy-start | bytes 49156
  27.4 6.5 %copy-start.4 = (bf16[24,3,512]{2,0,1:T(8,128)(2,1)S(1)}, bf16[24,3,512]{2,0,1:T(8,128)(2,1)}, u32[]{:S(2)}) copy-start(bf16[24,3,512]{2,0,1:T(8,128)(2,1)} %param.35) | copy-start | bytes 221188
  27.4 6.5 %copy-start.5 = (bf16[4,512]{1,0:T(4,128)(2,1)S(1)}, bf16[4,512]{1,0:T(4,128)(2,1)}, u32[]{:S(2)}) copy-start(bf16[4,512]{1,0:T(4,128)(2,1)} %param.25) | copy-start | bytes 12292
  27.4 6.5 %copy-start.6 = (bf16[512]{0:T(512)(128)(2,1)S(1)}, bf16[512]{0:T(512)(128)(2,1)}, u32[]{:S(2)}) copy-start(bf16[512]{0:T(512)(128)(2,1)} %param.26) | copy-start | bytes 3076
  32.7 1.9 %copy-start.11 = (bf16[4096,8]{0,1:T(8,128)(2,1)S(1)}, bf16[4096,8]{0,1:T(8,128)(2,1)}, u32[]{:S(2)}) copy-start(bf16[4096,8]{0,1:T(8,128)(2,1)} %param.24) | copy-start | bytes 196612
  32.8 1.9 %copy-start.13 = (f32[8]{0:T(128)S(1)}, f32[8]{0:T(128)}, u32[]{:S(2)}) copy-start(f32[8]{0:T(128)} %param.30) | copy-start | bytes 100
  32.8 1.9 %copy-start.14 = (f32[8]{0:T(128)S(1)}, f32[8]{0:T(128)}, u32[]{:S(2)}) copy-start(f32[8]{0:T(128)} %param.29) | copy-start | bytes 100
  37.2 13.7 %copy-start.2 = (f32[24,8]{1,0:T(8,128)}, f32[24,8]{1,0:T(8,128)S(1)}, u32[]{:S(2)}) copy-start(f32[24,8]{1,0:T(8,128)S(1)} %multiply_reduce_fusion.1) | copy-start | bytes 2308
  40.3 11.3 %copy-start.9 = (s32[24]{0:T(128)S(1)}, s32[24]{0:T(128)}, u32[]{:S(2)}) copy-start(s32[24]{0:T(128)} %param.38) | copy-start | bytes 292
  40.3 11.3 %copy-start.10 = (pred[24]{0:T(512)(128)(4,1)S(1)}, pred[24]{0:T(512)(128)(4,1)}, u32[]{:S(2)}) copy-start(pred[24]{0:T(512)(128)(4,1)} %broadcast_compare_fusion) | copy-start | bytes 76
  51.6 3.9 %collective-permute-start.1 = (f32[192]{0:T(256)}, f32[192]{0:T(256)}, u32[]{:S(2)}, u32[]{:S(2)}) collective-permute-start(f32[192]{0:T(256)} %reduce_sum.40), channel_id=1, source_target_pairs={{0,1},{1,0},{2,3},{3,2},{4,5},{5,4},{6,7},{7,6},{8,9},{9,8},{10,11... | collective-permute-start | bytes 2312 | tf_op jit(solution)/shard_map/ppermute | solution.py:13
  61.2 82.6 %copy-start.3 = (f32[24,8]{1,0:T(8,128)S(1)}, f32[24,8]{1,0:T(8,128)}, u32[]{:S(2)}) copy-start(f32[24,8]{1,0:T(8,128)} %copy-done.2) | copy-start | bytes 2308
  61.2 121.4 %all-gather.2.cloned.1.call-start = ((), (), s32[]{:S(2)}) async-start(), calls=%async_computation.2 | async-start | bytes 1769472 | tf_op jit(solution)/shard_map/all_gather | solution.py:139
Sparse Core Ops, SparseCore 0:
  61.4 75.1 reduce-scatter.1
  139.3 43.3 all-gather.1
where the time goes:
time: 193 us; the launch traced here: 192 us
  waiting for transfers between devices  98.5 us (51%)
  matrix products  40.2 us (21%)
  local copies, waits for them, and re-layouts  21.4 us (11%)
  between operations  14.4 us (7%)
  other arithmetic  8.99 us (5%)
  blocking collectives  5.55 us (3%)
  starting transfers between devices  3.18 us (2%)
    reduce_scatter x1, waiting for transfers between devices, local(): lax.psum_scatter(jnp.dot(normalized, out_weight, preferred_element_type=j...  75.3 us
    all_gather x1, waiting for transfers between devices, local(): layer_rows = lax.all_gather(own_rows, 'tensor', axis=0, tiled=True)  22.4 us
    dot_general x1, matrix products, local(): jnp.einsum('rjhp,rjn->rhpn', weighted, input_map, precision=HIGHEST_PRECI...  13.1 us
    unnamed x34, local copies, waits for them, and re-layouts  12.9 us
    dot_general x1, matrix products, local(): jnp.einsum('rhpn,rsn->rshp', initial, output_map, precision=HIGHEST_PRECI...  10.6 us
    psum x1, blocking collectives, local(): accepted_total = lax.psum(jnp.sum(kept_count), 'dp').reshape(1)  5.55 us
    dot_general x1, matrix products, local(): inner_sum = jnp.dot(normed, in_flat, preferred_element_type=jnp.float32)  5.31 us
    dot_general x1, matrix products, local(): jnp.dot(normalized, out_weight, preferred_element_type=jnp.float32)  5.08 us
  transfers between devices with their start and end apart: 4, of which 3 were waited for; matrix products, arithmetic and copies ran while one was open for 21% of the time, Pallas kernels for 0%

commit v1 on v0

--- a/solution.py
+++ b/solution.py
@@ -1,16 +1,30 @@
 import jax
 import jax.numpy as jnp
 from jax import lax
+from jax.experimental import pallas as pl
+from jax.experimental.pallas import tpu as pltpu
 from jax.sharding import PartitionSpec as P
 
 EPSILON = 1e-05
-HIGHEST_PRECISION = lax.Precision.HIGHEST
+
+
+def narrow(value):
+    return value.astype(jnp.bfloat16)
 
 
 def swapped(value, axis, distance):
     mask = 2**distance
     pairs = [(source, source ^ mask) for source in range(lax.axis_size(axis))]
     return lax.ppermute(value, axis, pairs)
+
+
+def total_over_dp(own):
+    members = lax.axis_size("dp")
+    total = own
+    for hop in range(1, members):
+        pairs = [(source, (source + hop) % members) for source in range(members)]
+        total = total + lax.ppermute(own, "dp", pairs)
+    return total
 
 
 def convolve(window, fresh_rows, kernel, offset):
@@ -28,6 +42,157 @@
     return jax.vmap(
         lambda single, start_row: lax.dynamic_slice_in_dim(single, start_row, width_rows, 0)
     )(sequence, kept_count)
+
+
+MESH = pl.DeviceIdType.MESH
+
+
+def project_kernel(
+    normalized_ref,
+    weight_ref,
+    out_ref,
+    weight_buf,
+    pair_send,
+    pair_recv,
+    far_send,
+    far_recv,
+    kept_acc,
+    weight_sem,
+    pair_sems,
+    far_sems,
+    pair_out_sems,
+    far_out_sems,
+):
+    members = lax.axis_size("tensor")
+    fars = members // 2
+    me = lax.axis_index("tensor")
+    far, near = me // 2, me % 2
+    partner = far * 2 + (1 - near)
+    width = out_ref.shape[1] // members
+
+    def far_at(step):
+        return lax.rem(far + 1 + step, fars)
+
+    def columns(block):
+        return pl.ds(pl.multiple_of(block * width, width), width)
+
+    order = [far_at(step) * 2 + (1 - near) for step in range(fars)]
+    order += [far_at(step) * 2 + near for step in range(fars)]
+    loads = [
+        pltpu.make_async_copy(
+            weight_ref.at[:, columns(block)], weight_buf.at[slot], weight_sem.at[slot]
+        )
+        for slot, block in enumerate(order)
+    ]
+    for load in loads:
+        load.start()
+
+    barrier = pltpu.get_barrier_semaphore()
+    pl.semaphore_signal(barrier, inc=1, device_id={"tensor": partner}, device_id_type=MESH)
+    for step in range(fars - 1):
+        pl.semaphore_signal(
+            barrier, inc=1, device_id={"tensor": far_at(step) * 2 + near}, device_id_type=MESH
+        )
+    pl.semaphore_wait(barrier, fars)
+
+    def product(slot):
+        loads[slot].wait()
+        return jnp.dot(
+            normalized_ref[...], weight_buf[slot], preferred_element_type=jnp.float32
+        )
+
+    def remote(source, target, sems, index, device):
+        return pltpu.make_async_remote_copy(
+            src_ref=source,
+            dst_ref=target,
+            send_sem=sems.at[0, index],
+            recv_sem=sems.at[1, index],
+            device_id={"tensor": device},
+            device_id_type=MESH,
+        )
+
+    pair_copies = []
+    for step in range(fars):
+        pair_send[step] = product(step).astype(pair_send.dtype)
+        copy = remote(pair_send.at[step], pair_recv.at[step], pair_sems, step, partner)
+        copy.start()
+        pair_copies.append(copy)
+    far_copies = []
+    for step in range(fars):
+        summed = product(fars + step)
+        pair_copies[step].wait_recv()
+        summed = summed + pair_recv[step].astype(jnp.float32)
+        if step < fars - 1:
+            far_send[step] = summed.astype(far_send.dtype)
+            copy = remote(
+                far_send.at[step],
+                far_recv.at[step],
+                far_sems,
+                step,
+                far_at(step) * 2 + near,
+            )
+            copy.start()
+            far_copies.append(copy)
+        else:
+            kept_acc[...] = summed
+    for step in range(fars - 1):
+        far_copies[step].wait_recv()
+        kept_acc[...] += far_recv[step].astype(jnp.float32)
+    mine = out_ref.at[:, columns(me)]
+    out_ref[:, columns(me)] = kept_acc[...].astype(out_ref.dtype)
+    own = remote(mine, mine, pair_out_sems, 0, partner)
+    own.start()
+    far_outs = []
+    for step in range(fars - 1):
+        copy = remote(mine, mine, far_out_sems, step, far_at(step) * 2 + near)
+        copy.start()
+        far_outs.append(copy)
+    pair_outs = [own]
+    for step in range(fars - 1):
+        far_outs[step].wait_recv()
+        source = lax.rem(far - 1 - step + 2 * fars, fars) * 2 + near
+        there = out_ref.at[:, columns(source)]
+        copy = remote(there, there, pair_out_sems, step + 1, partner)
+        copy.start()
+        pair_outs.append(copy)
+    for copy in pair_outs:
+        copy.wait_recv()
+    for copy in pair_copies + far_copies + far_outs + pair_outs:
+        copy.wait_send()
+
+
+def project(normalized, out_weight):
+    rows, inner = normalized.shape
+    model_width = out_weight.shape[1]
+    members = lax.axis_size("tensor")
+    fars = members // 2
+    width = model_width // members
+    block = (rows, width)
+    return pl.pallas_call(
+        project_kernel,
+        out_shape=jax.ShapeDtypeStruct((rows, model_width), jnp.bfloat16),
+        in_specs=[
+            pl.BlockSpec(memory_space=pltpu.VMEM),
+            pl.BlockSpec(memory_space=pl.ANY),
+        ],
+        out_specs=pl.BlockSpec(memory_space=pltpu.VMEM),
+        scratch_shapes=[
+            pltpu.VMEM((members, inner, width), jnp.bfloat16),
+            pltpu.VMEM((fars, *block), jnp.bfloat16),
+            pltpu.VMEM((fars, *block), jnp.bfloat16),
+            pltpu.VMEM((fars - 1, *block), jnp.bfloat16),
+            pltpu.VMEM((fars - 1, *block), jnp.bfloat16),
+            pltpu.VMEM(block, jnp.float32),
+            pltpu.SemaphoreType.DMA((members,)),
+            pltpu.SemaphoreType.DMA((2, fars)),
+            pltpu.SemaphoreType.DMA((2, fars - 1)),
+            pltpu.SemaphoreType.DMA((2, fars)),
+            pltpu.SemaphoreType.DMA((2, fars - 1)),
+        ],
+        compiler_params=pltpu.CompilerParams(
+            collective_id=0, has_side_effects=True, vmem_limit_bytes=40 * 1024 * 1024
+        ),
+    )(normalized, out_weight)
 
 
 def local(
@@ -59,7 +224,7 @@
     head_dim = inner_dev // head_count
     tap_count = value_kernel.shape[0]
     kept_count = accepted * live_flags
-    accepted_total = lax.psum(jnp.sum(kept_count), "dp").reshape(1)
+    accepted_total = total_over_dp(jnp.sum(kept_count).reshape(1))
     flat_rows = tokens.reshape(row_total, model_width).astype(jnp.float32)
     normed = (
         flat_rows
@@ -87,7 +252,7 @@
         [jnp.zeros((requests, 1, head_count), jnp.float32), jnp.cumsum(log_decay, axis=1)], axis=1
     )
     after_step = prefix[:, 1:]
-    alignment = jnp.einsum("rsn,rjn->rsj", output_map, input_map, precision=HIGHEST_PRECISION)
+    alignment = jnp.einsum("rsn,rjn->rsj", narrow(output_map), narrow(input_map), preferred_element_type=jnp.float32)
     causal = (jnp.arange(positions)[:, None] >= jnp.arange(positions)[None, :])[None, :, :, None]
     spread = after_step[:, :, None, :] - after_step[:, None, :, :]
     weights_mix = (
@@ -95,10 +260,10 @@
         * step_size[:, None, :, :]
         * alignment[:, :, :, None]
     )
-    within = jnp.einsum("rsjh,rjhp->rshp", weights_mix, values, precision=HIGHEST_PRECISION)
+    within = jnp.einsum("rsjh,rjhp->rshp", narrow(weights_mix), narrow(values), preferred_element_type=jnp.float32)
     initial = scan_state.astype(jnp.float32)
     carried = (
-        jnp.einsum("rhpn,rsn->rshp", initial, output_map, precision=HIGHEST_PRECISION)
+        jnp.einsum("rhpn,rsn->rshp", scan_state, narrow(output_map), preferred_element_type=jnp.float32)
         * jnp.exp(after_step)[:, :, :, None]
     )
     head_out = within + carried + skip_gain[:, None] * values
@@ -116,7 +281,7 @@
     weighted = keep_weight[:, :, :, None] * values
     kept_state = (
         jnp.exp(prefix_kept)[:, :, None, None] * initial
-        + jnp.einsum("rjhp,rjn->rhpn", weighted, input_map, precision=HIGHEST_PRECISION)
+        + jnp.einsum("rjhp,rjn->rhpn", narrow(weighted), narrow(input_map), preferred_element_type=jnp.float32)
     ).astype(jnp.bfloat16)
     gated = head_out.reshape(row_total, inner_dev) * jax.nn.silu(
         gate_part.reshape(row_total, inner_dev).astype(jnp.float32)
@@ -130,13 +295,7 @@
     normalized = jnp.where(
         valid_rows.reshape(row_total, 1), gated * scale_rows[:, None] * out_gain, 0.0
     ).astype(jnp.bfloat16)
-    own_rows = lax.psum_scatter(
-        jnp.dot(normalized, out_weight, preferred_element_type=jnp.float32),
-        "tensor",
-        scatter_dimension=0,
-        tiled=True,
-    ).astype(jnp.bfloat16)
-    layer_rows = lax.all_gather(own_rows, "tensor", axis=0, tiled=True)
+    layer_rows = project(normalized, out_weight)
     value_kept = keep_window(value_seq, kept_count, tap_count - 1)
     group_kept = keep_window(group_seq, kept_count, tap_count - 1)
     return (

time: 193 us -> 121 us (0.63)
  the two profiles are of different devices: /device:TPU:0 before, /device:TPU:22 now
where the time goes in v1:
time: 121 us
  Pallas kernels  55.4 us (46%)
  local copies, waits for them, and re-layouts  23.3 us (19%)
  matrix products  21.1 us (17%)
  other arithmetic  11.9 us (10%)
  between operations  4.87 us (4%)
  starting transfers between devices  4.1 us (3%)
    pallas_call x1, Pallas kernels, project(): pl.pallas_call(project_kernel, out_shape=jax.ShapeDtypeStruct((rows, mode...  55.4 us
    unnamed x48, local copies, waits for them, and re-layouts  13.7 us
    dot_general x1, matrix products, local(): jnp.einsum('rjhp,rjn->rhpn', narrow(weighted), narrow(input_map), preferr...  5.54 us
    dot_general x1, matrix products, local(): inner_sum = jnp.dot(normed, in_flat, preferred_element_type=jnp.float32)  5.3 us
    dot_general x1, matrix products, local(): jnp.einsum('rhpn,rsn->rshp', scan_state, narrow(output_map), preferred_el...  4.42 us
    gather x2, local copies, waits for them, and re-layouts, keep_window(): lax.dynamic_slice_in_dim(single, start_row, width_rows, 0)  3.05 us
  transfers between devices with their start and end apart: 5, of which 0 were waited for; matrix products, arithmetic and copies ran while one was open for 37% of the time, Pallas kernels for 0%

profile of v1, /device:TPU:22, one launch (start us, length us, event | category | flops | bytes accessed | tf_op | source)
XLA Modules:
  0.0 120.7 jit_solution(7394071432018734914)
XLA Ops:
  0.7 1.4 %fusion.64 = (s32[]{:T(128)}, s32[24]{0:T(128)S(1)}) fusion(s32[24]{0:T(128)} %param.37, s32[24]{0:T(128)} %param.39), kind=kLoop, calls=%fused_computation.93 | loop fusion | flops 47 | bytes 292 | tf_op jit(solution)/shard_map/reduce_sum | solution.py:227
  2.6 1.5 %collective-permute-start.4 = (s32[1]{0:T(128)}, s32[1]{0:T(128)}, u32[]{:S(2)}, u32[]{:S(2)}) collective-permute-start(s32[1]{0:T(128)} %bitcast.22), channel_id=1, source_target_pairs={{0,24},{8,0},{16,8},{24,16},{1,25},{9,1},{17,9},{25,17},{2,26},{10... | collective-permute-start | bytes 20 | tf_op jit(solution)/shard_map/ppermute | solution.py:26
  4.1 1.8 %fusion = f32[24,8]{1,0:T(8,128)S(1)} fusion(bf16[24,8,4096]{2,1,0:T(8,128)(2,1)} %param.20), kind=kLoop, calls=%fused_computation.6 | loop fusion | flops 2359104 | bytes 1573632 | tf_op jit(solution)/shard_map/reduce_sum | solution.py:231
  6.7 0.8 bitcast_convert_fusion.3
  8.2 2.1 %fusion.29 = bf16[24,8,128]{2,1,0:T(8,128)(2,1)S(1)} fusion(bf16[4096,128]{1,0:T(8,128)(2,1)S(1)} %copy-done, bf16[24,8,4096]{2,1,0:T(8,128)(2,1)} %param.20, f32[4096]{0:T(1024)} %param.21, f32[192]{0:T(256)S(1)} %rsqrt.16), kind=kOutput, calls=%fused_computation.26 | convolution fusion | flops 204496896 | bytes 2687744 | tf_op jit(solution)/shard_map/dot_general | solution.py:237
  12.7 9.5 %copy.55 = bf16[512,8,2,512]{3,1,2,0:T(8,128)(2,1)} copy(bf16[512,8,2,512]{3,2,1,0:T(2,128)(2,1)} %bitcast.98) | data formatting | bytes 16777216
  22.2 5.3 %fusion.17 = bf16[24,8,1024]{2,1,0:T(8,128)(2,1)S(1)} fusion(bf16[4096,1024]{1,0:T(8,128)(2,1)} %bitcast.99, bf16[24,8,4096]{2,1,0:T(8,128)(2,1)S(1)} %copy-done.2, f32[4096]{0:T(1024)S(1)} %copy-done.17, f32[24,8]{1,0:T(8,128)S(1)} %add_rsqrt_fusion), kind=kOutput, calls=%fused_computation.22 | convolution fusion | flops 1613955072 | bytes 10371840 | tf_op jit(solution)/shard_map/dot_general | solution.py:236
  28.4 2.1 %negate_multiply_fusion = (f32[24,8,8]{2,1,0:T(8,128)S(1)}, f32[24,8,8]{2,1,0:T(8,128)S(1)}) fusion(f32[8]{0:T(128)S(1)} %copy-done.18, f32[8]{0:T(128)S(1)} %copy-done.19, bf16[4096,8]{0,1:T(8,128)(2,1)S(1)} %copy-done.16, bf16[24,8,4096]{2,1,0:T(8,128)(2,1)} %param.20, f32[4096]{0:T(1024)S(1)} %copy-done.17, f32[24,8]{1,0:T(8,128)S(1)} %add_rsqrt_fusion), kind=kOutput, calls=%fused_computation.57 | convolution fusion | flops 15742464 | bytes 1667904 | tf_op jit(solution)/shard_map/dot_general | solution.py:238
  31.5 1.0 multiply_convert_fusion
  32.6 1.3 %fusion.56 = pred[24,8]{1,0:T(8,128)(4,1)} fusion(s32[24]{0:T(128)} %param.38, pred[24]{0:T(512)(128)(4,1)} %broadcast_compare_fusion), kind=kLoop, calls=%fused_computation.71 | loop fusion | flops 384 | bytes 312 | tf_op jit(solution)/shard_map/and | solution.py:292
  34.5 1.6 %copy.40 = f32[24,8,8]{1,2,0:T(8,128)} copy(f32[24,8,8]{2,1,0:T(8,128)} %copy-done.5) | data formatting | bytes 12288 | tf_op jit(solution)/shard_map/jit(softplus)/select_n | solution.py:249
  36.8 1.3 %exp.46 = f32[24,8]{1,0:T(8,128)} exponential(f32[24,8]{1,0:T(8,128)} %copy-done.7) | non-fusion elementwise | bytes 1536 | tf_op jit(solution)/shard_map/exp | solution.py:283
  38.2 1.6 %gather_fusion = bf16[24,3,512]{2,0,1:T(8,128)(2,1)} fusion(bf16[24,11,512]{2,0,1:T(8,128)(2,1)S(1)} %copy_dynamic-update-slice_fusion, s32[24]{0:T(128)S(1)} %fusion.62), kind=kCustom, calls=%fused_computation | custom fusion | bytes 147744 | tf_op jit(solution)/shard_map/vmap()/gather | solution.py:43
  39.8 1.4 %gather_fusion.1 = bf16[24,3,128]{2,0,1:T(8,128)(2,1)} fusion(bf16[24,11,128]{2,0,1:T(8,128)(2,1)S(1)} %copy_dynamic-update-slice_fusion.1, s32[24]{0:T(128)S(1)} %fusion.62), kind=kCustom, calls=%fused_computation.1 | custom fusion | bytes 37152 | tf_op jit(solution)/shard_map/vmap()/gather | solution.py:43
  41.2 1.1 reshape.253
  42.4 0.8 and.23
  45.9 0.8 select_convert_fusion.1
  46.9 4.4 %convolution_multiply_fusion = f32[24,8,8,64]{3,1,2,0:T(8,128)S(1)} fusion(bf16[24,8,64,128]{3,2,1,0:T(8,128)(2,1)} %param.34, f32[24,8,8]{1,2,0:T(8,128)S(1)} %copy.45, bf16[24,8,128]{2,0,1:T(8,128)(2,1)S(1)} %get-tuple-element.14), kind=kOutput, calls=%fused_computation.20 | convolution fusion | flops 25264128 | bytes 3594240 | tf_op jit(solution)/shard_map/rhpn,rsn->rshp/dot_general | solution.py:266
  51.4 1.6 %multiply_reduce_fusion = (f32[24,8]{1,0:T(8,128)S(1)}, f32[24,8,8,64]{3,1,2,0:T(8,128)}) fusion(f32[24,8,8,64]{3,2,1,0:T(8,128)S(1)} %copy-done.3, f32[24,8,8,64]{3,2,1,0:T(8,128)S(1)} %reshape.238, f32[8]{0:T(128)S(1)} %copy-done.20, f32[24,8,8,64]{3,1,2,0:T(8,128)S(1)} %convolution_multiply_fusion, f32[24,8,8]{2,1,0:T(8,128)S(1)} %fusion.51, ...), kind=kOutput, calls=%fused_computation.29 | convolution fusion | flops 2629440 | bytes 1788768 | tf_op jit(solution)/shard_map/rsjh,rjhp->rshp/dot_general | solution.py:263
  53.1 1.6 %collective-permute-start.1 = (f32[192]{0:T(256)S(1)}, f32[192]{0:T(256)S(1)}, u32[]{:S(2)}, u32[]{:S(2)}) collective-permute-start(f32[192]{0:T(256)S(1)} %reduce_sum.40), channel_id=1, source_target_pairs={{0,1},{1,0},{2,3},{3,2},{4,5},{5,4},{6,7},{7,6},{8,9},{9,8},{10,11... | collective-permute-start | bytes 2312 | tf_op jit(solution)/shard_map/ppermute | solution.py:18
  54.7 5.5 %add_convert_fusion = bf16[24,8,64,128]{3,2,1,0:T(8,128)(2,1)} fusion(bf16[24,8,64,128]{3,2,1,0:T(8,128)(2,1)} %param.34, f32[24,8]{1,0:T(8,128)S(1)} %copy-done.11, bf16[24,8,8,64]{3,2,1,0:T(8,128)(2,1)S(1)} %get-tuple-element.7, bf16[24,8,128]{2,0,1:T(8,128)(2,1)S(1)} %get-tuple-element.13), kind=kOutput, calls=%fused_computation.2 | convolution fusion | flops 31457280 | bytes 6537984 | tf_op jit(solution)/shard_map/rjhp,rjn->rhpn/dot_general | solution.py:284
  60.8 2.2 %copy-done.1 = bf16[512,4096]{1,0:T(8,128)(2,1)S(1)} copy-done((bf16[512,4096]{1,0:T(8,128)(2,1)S(1)}, bf16[512,4096]{1,0:T(8,128)(2,1)}, u32[]{:S(2)}) %copy-start.1) | copy-done | bytes 4194328
  63.0 55.4 %shard_map.227 = bf16[192,4096]{1,0:T(8,128)(2,1)S(1)} custom-call(bf16[192,512]{1,0:T(8,128)(2,1)S(1)} %select_convert_fusion.normalized_ref, bf16[512,4096]{1,0:T(8,128)(2,1)S(1)} %copy-done.1), custom_call_target="tpu_custom_call" | custom-call | tf_op jit(solution)/shard_map/pallas_call | solution.py:171
  118.4 1.1 copy.85
  (81 shorter events, 8.5 us)
Async XLA Ops:
  0.6 7.5 %copy-start = (bf16[4096,128]{1,0:T(8,128)(2,1)S(1)}, bf16[4096,128]{1,0:T(8,128)(2,1)}, u32[]{:S(2)}) copy-start(bf16[4096,128]{1,0:T(8,128)(2,1)} %param.23) | copy-start | bytes 3145732
  0.6 11.5 %copy-start.15 = (s32[24]{0:T(128)S(1)}, s32[24]{0:T(128)}, u32[]{:S(2)}) copy-start(s32[24]{0:T(128)} %param.39) | copy-start | bytes 292
  2.1 41.1 %collective-permute-start.2 = (s32[1]{0:T(128)}, s32[1]{0:T(128)}, u32[]{:S(2)}, u32[]{:S(2)}) collective-permute-start(s32[1]{0:T(128)} %bitcast.22), channel_id=1, source_target_pairs={{0,8},{8,16},{16,24},{24,0},{1,9},{9,17},{17,25},{25,1},{2,10},{10... | collective-permute-start | bytes 20 | tf_op jit(solution)/shard_map/ppermute | solution.py:26
  2.1 42.5 %collective-permute-start.3 = (s32[1]{0:T(128)}, s32[1]{0:T(128)}, u32[]{:S(2)}, u32[]{:S(2)}) collective-permute-start(s32[1]{0:T(128)} %bitcast.22), channel_id=1, source_target_pairs={{0,16},{8,24},{16,0},{24,8},{1,17},{9,25},{17,1},{25,9},{2,18},{10... | collective-permute-start | bytes 20 | tf_op jit(solution)/shard_map/ppermute | solution.py:26
  2.6 42.6 %collective-permute-start.4 = (s32[1]{0:T(128)}, s32[1]{0:T(128)}, u32[]{:S(2)}, u32[]{:S(2)}) collective-permute-start(s32[1]{0:T(128)} %bitcast.22), channel_id=1, source_target_pairs={{0,24},{8,0},{16,8},{24,16},{1,25},{9,1},{17,9},{25,17},{2,26},{10... | collective-permute-start | bytes 20 | tf_op jit(solution)/shard_map/ppermute | solution.py:26
  10.9 34.9 %collective-permute-start = (bf16[24,8,128]{2,0,1:T(8,128)(2,1)}, bf16[24,8,128]{2,0,1:T(8,128)(2,1)}, u32[]{:S(2)}, u32[]{:S(2)}) collective-permute-start(bf16[24,8,128]{2,0,1:T(8,128)(2,1)} %divide_multiply_fusion.1), channel_id=1, source_target_pairs={{0,1},{1,0},{2,3},{3,2},{4,5},{5,4},{6,7},{7,6},{8,9},{9,8},{10,11... | collective-permute-start | bytes 147464 | tf_op jit(solution)/shard_map/ppermute | solution.py:18
  12.7 9.5 %copy-start.2 = (bf16[24,8,4096]{2,1,0:T(8,128)(2,1)S(1)}, bf16[24,8,4096]{2,1,0:T(8,128)(2,1)}, u32[]{:S(2)}) copy-start(bf16[24,8,4096]{2,1,0:T(8,128)(2,1)} %param.20) | copy-start | bytes 4718596
  12.7 9.5 %copy-start.17 = (f32[4096]{0:T(1024)S(1)}, f32[4096]{0:T(1024)}, u32[]{:S(2)}) copy-start(f32[4096]{0:T(1024)} %param.21) | copy-start | bytes 49156
  22.1 5.4 %copy-start.10 = (bf16[24,3,512]{2,0,1:T(8,128)(2,1)S(1)}, bf16[24,3,512]{2,0,1:T(8,128)(2,1)}, u32[]{:S(2)}) copy-start(bf16[24,3,512]{2,0,1:T(8,128)(2,1)} %param.35) | copy-start | bytes 221188
  22.1 5.4 %copy-start.12 = (bf16[4,512]{1,0:T(4,128)(2,1)S(1)}, bf16[4,512]{1,0:T(4,128)(2,1)}, u32[]{:S(2)}) copy-start(bf16[4,512]{1,0:T(4,128)(2,1)} %param.25) | copy-start | bytes 12292
  22.2 5.5 %copy-start.14 = (bf16[512]{0:T(512)(128)(2,1)S(1)}, bf16[512]{0:T(512)(128)(2,1)}, u32[]{:S(2)}) copy-start(bf16[512]{0:T(512)(128)(2,1)} %param.26) | copy-start | bytes 3076
  27.5 0.9 copy-start.16
  30.5 1.1 copy-start.5
  39.8 11.5 %copy-start.8 = (f32[24,8,8]{1,2,0:T(8,128)S(1)}, f32[24,8,8]{1,2,0:T(8,128)}, u32[]{:S(2)}) copy-start(f32[24,8,8]{1,2,0:T(8,128)} %copy.40) | copy-start | bytes 18436
  39.8 11.5 %copy-start.9 = (f32[24,8,8]{1,2,0:T(8,128)S(1)}, f32[24,8,8]{1,2,0:T(8,128)}, u32[]{:S(2)}) copy-start(f32[24,8,8]{1,2,0:T(8,128)} %copy.38) | copy-start | bytes 18436
  39.8 11.5 %copy-start.20 = (f32[8]{0:T(128)S(1)}, f32[8]{0:T(128)}, u32[]{:S(2)}) copy-start(f32[8]{0:T(128)} %param.31) | copy-start | bytes 100
  39.8 11.6 %copy-start.21 = (pred[8,8]{1,0:T(8,128)(4,1)S(1)}, pred[8,8]{1,0:T(8,128)(4,1)}, u32[]{:S(2)}) copy-start(pred[8,8]{1,0:T(8,128)(4,1)} %iota_compare_fusion.3) | copy-start | bytes 196
  42.3 9.1 %copy-start.6 = (bf16[24,8,8,64]{3,2,1,0:T(8,128)(2,1)S(1)}, bf16[24,8,8,64]{3,2,1,0:T(8,128)(2,1)}, u32[]{:S(2)}) copy-start(bf16[24,8,8,64]{3,2,1,0:T(8,128)(2,1)} %get-tuple-element.8) | copy-start | bytes 589828
  43.2 8.2 %copy-start.3 = (f32[24,8,8,64]{3,2,1,0:T(8,128)S(1)}, f32[24,8,8,64]{3,2,1,0:T(8,128)}, u32[]{:S(2)}) copy-start(f32[24,8,8,64]{3,2,1,0:T(8,128)} %reshape.253) | copy-start | bytes 1179652
  51.4 3.3 %copy-start.11 = (f32[24,8]{1,0:T(8,128)S(1)}, f32[24,8]{1,0:T(8,128)}, u32[]{:S(2)}) copy-start(f32[24,8]{1,0:T(8,128)} %exp.46) | copy-start | bytes 2308
  53.1 7.5 %collective-permute-start.1 = (f32[192]{0:T(256)S(1)}, f32[192]{0:T(256)S(1)}, u32[]{:S(2)}, u32[]{:S(2)}) collective-permute-start(f32[192]{0:T(256)S(1)} %reduce_sum.40), channel_id=1, source_target_pairs={{0,1},{1,0},{2,3},{3,2},{4,5},{5,4},{6,7},{7,6},{8,9},{9,8},{10,11... | collective-permute-start | bytes 2312 | tf_op jit(solution)/shard_map/ppermute | solution.py:18
  54.7 5.5 %copy-start.4 = (f32[24,8,8,64]{3,1,2,0:T(8,128)S(1)}, f32[24,8,8,64]{3,1,2,0:T(8,128)}, u32[]{:S(2)}) copy-start(f32[24,8,8,64]{3,1,2,0:T(8,128)} %get-tuple-element.26) | copy-start | bytes 1179652
  54.7 5.9 %copy-start.13 = (f32[512]{0:T(512)S(1)}, f32[512]{0:T(512)}, u32[]{:S(2)}) copy-start(f32[512]{0:T(512)} %param.32) | copy-start | bytes 6148
  60.8 2.2 %copy-start.1 = (bf16[512,4096]{1,0:T(8,128)(2,1)S(1)}, bf16[512,4096]{1,0:T(8,128)(2,1)}, u32[]{:S(2)}) copy-start(bf16[512,4096]{1,0:T(8,128)(2,1)} %weight_ref.1) | copy-start | bytes 12582916
  (3 other events, 2.6 us)

commit v2 on v1

--- a/solution.py
+++ b/solution.py
@@ -16,15 +16,6 @@
     mask = 2**distance
     pairs = [(source, source ^ mask) for source in range(lax.axis_size(axis))]
     return lax.ppermute(value, axis, pairs)
-
-
-def total_over_dp(own):
-    members = lax.axis_size("dp")
-    total = own
-    for hop in range(1, members):
-        pairs = [(source, (source + hop) % members) for source in range(members)]
-        total = total + lax.ppermute(own, "dp", pairs)
-    return total
 
 
 def convolve(window, fresh_rows, kernel, offset):
@@ -39,9 +30,11 @@
 
 
 def keep_window(sequence, kept_count, width_rows):
-    return jax.vmap(
-        lambda single, start_row: lax.dynamic_slice_in_dim(single, start_row, width_rows, 0)
-    )(sequence, kept_count)
+    kept = sequence[:, :width_rows]
+    for start_row in range(1, sequence.shape[1] - width_rows + 1):
+        chosen = (kept_count == start_row)[:, None, None]
+        kept = jnp.where(chosen, sequence[:, start_row : start_row + width_rows], kept)
+    return kept
 
 
 MESH = pl.DeviceIdType.MESH
@@ -50,18 +43,22 @@
 def project_kernel(
     normalized_ref,
     weight_ref,
+    count_ref,
     out_ref,
+    total_ref,
     weight_buf,
     pair_send,
     pair_recv,
     far_send,
     far_recv,
     kept_acc,
+    count_recv,
     weight_sem,
     pair_sems,
     far_sems,
     pair_out_sems,
     far_out_sems,
+    count_sems,
 ):
     members = lax.axis_size("tensor")
     fars = members // 2
@@ -69,6 +66,9 @@
     far, near = me // 2, me % 2
     partner = far * 2 + (1 - near)
     width = out_ref.shape[1] // members
+    groups = lax.axis_size("dp")
+    group = lax.axis_index("dp")
+    parts, height = kept_acc.shape[:2]
 
     def far_at(step):
         return lax.rem(far + 1 + step, fars)
@@ -93,12 +93,22 @@
         pl.semaphore_signal(
             barrier, inc=1, device_id={"tensor": far_at(step) * 2 + near}, device_id_type=MESH
         )
-    pl.semaphore_wait(barrier, fars)
-
-    def product(slot):
-        loads[slot].wait()
+    for hop in range(groups - 1):
+        pl.semaphore_signal(
+            barrier,
+            inc=1,
+            device_id={"dp": lax.rem(group + 1 + hop, groups)},
+            device_id_type=MESH,
+        )
+    pl.semaphore_wait(barrier, fars + groups - 1)
+
+    def product(part, slot):
+        if part == 0:
+            loads[slot].wait()
         return jnp.dot(
-            normalized_ref[...], weight_buf[slot], preferred_element_type=jnp.float32
+            normalized_ref[part * height : (part + 1) * height],
+            weight_buf[slot],
+            preferred_element_type=jnp.float32,
         )
 
     def remote(source, target, sems, index, device):
@@ -111,88 +121,123 @@
             device_id_type=MESH,
         )
 
-    pair_copies = []
-    for step in range(fars):
-        pair_send[step] = product(step).astype(pair_send.dtype)
-        copy = remote(pair_send.at[step], pair_recv.at[step], pair_sems, step, partner)
+    count_copies = []
+    for hop in range(groups - 1):
+        copy = pltpu.make_async_remote_copy(
+            src_ref=count_ref,
+            dst_ref=count_recv.at[hop],
+            send_sem=count_sems.at[0, hop],
+            recv_sem=count_sems.at[1, hop],
+            device_id={"dp": lax.rem(group + 1 + hop, groups)},
+            device_id_type=MESH,
+        )
         copy.start()
-        pair_copies.append(copy)
-    far_copies = []
-    for step in range(fars):
-        summed = product(fars + step)
-        pair_copies[step].wait_recv()
-        summed = summed + pair_recv[step].astype(jnp.float32)
-        if step < fars - 1:
-            far_send[step] = summed.astype(far_send.dtype)
-            copy = remote(
-                far_send.at[step],
-                far_recv.at[step],
-                far_sems,
-                step,
-                far_at(step) * 2 + near,
-            )
+        count_copies.append(copy)
+
+    pair_copies, far_copies, pair_outs, far_outs = [], [], [], []
+    for part in range(parts):
+        for step in range(fars):
+            slot = part * fars + step
+            pair_send[slot] = product(part, step).astype(pair_send.dtype)
+            copy = remote(pair_send.at[slot], pair_recv.at[slot], pair_sems, slot, partner)
             copy.start()
-            far_copies.append(copy)
-        else:
-            kept_acc[...] = summed
-    for step in range(fars - 1):
-        far_copies[step].wait_recv()
-        kept_acc[...] += far_recv[step].astype(jnp.float32)
-    mine = out_ref.at[:, columns(me)]
-    out_ref[:, columns(me)] = kept_acc[...].astype(out_ref.dtype)
-    own = remote(mine, mine, pair_out_sems, 0, partner)
-    own.start()
-    far_outs = []
-    for step in range(fars - 1):
-        copy = remote(mine, mine, far_out_sems, step, far_at(step) * 2 + near)
-        copy.start()
-        far_outs.append(copy)
-    pair_outs = [own]
-    for step in range(fars - 1):
-        far_outs[step].wait_recv()
-        source = lax.rem(far - 1 - step + 2 * fars, fars) * 2 + near
-        there = out_ref.at[:, columns(source)]
-        copy = remote(there, there, pair_out_sems, step + 1, partner)
+            pair_copies.append(copy)
+    for part in range(parts):
+        for step in range(fars):
+            summed = product(part, fars + step)
+            pair_copies[part * fars + step].wait_recv()
+            summed = summed + pair_recv[part * fars + step].astype(jnp.float32)
+            if step < fars - 1:
+                slot = part * (fars - 1) + step
+                far_send[slot] = summed.astype(far_send.dtype)
+                copy = remote(
+                    far_send.at[slot],
+                    far_recv.at[slot],
+                    far_sems,
+                    slot,
+                    far_at(step) * 2 + near,
+                )
+                copy.start()
+                far_copies.append(copy)
+            else:
+                kept_acc[part] = summed
+    for part in range(parts):
+        rows = pl.ds(part * height, height)
+        total = kept_acc[part]
+        for step in range(fars - 1):
+            slot = part * (fars - 1) + step
+            far_copies[slot].wait_recv()
+            total = total + far_recv[slot].astype(jnp.float32)
+        mine = out_ref.at[rows, columns(me)]
+        out_ref[rows, columns(me)] = total.astype(out_ref.dtype)
+        copy = remote(mine, mine, pair_out_sems, part * fars, partner)
         copy.start()
         pair_outs.append(copy)
+        for step in range(fars - 1):
+            slot = part * (fars - 1) + step
+            copy = remote(mine, mine, far_out_sems, slot, far_at(step) * 2 + near)
+            copy.start()
+            far_outs.append(copy)
+    for part in range(parts):
+        rows = pl.ds(part * height, height)
+        for step in range(fars - 1):
+            far_outs[part * (fars - 1) + step].wait_recv()
+            source = lax.rem(far - 1 - step + 2 * fars, fars) * 2 + near
+            there = out_ref.at[rows, columns(source)]
+            copy = remote(there, there, pair_out_sems, part * fars + step + 1, partner)
+            copy.start()
+            pair_outs.append(copy)
+    count = count_ref[...]
+    for hop in range(groups - 1):
+        count_copies[hop].wait_recv()
+        count = count + count_recv[hop]
+    total_ref[...] = count
     for copy in pair_outs:
         copy.wait_recv()
-    for copy in pair_copies + far_copies + far_outs + pair_outs:
+    for copy in pair_copies + far_copies + far_outs + pair_outs + count_copies:
         copy.wait_send()
 
 
-def project(normalized, out_weight):
+def project(normalized, out_weight, own_total):
     rows, inner = normalized.shape
     model_width = out_weight.shape[1]
     members = lax.axis_size("tensor")
+    groups = lax.axis_size("dp")
     fars = members // 2
+    parts = 2 if rows % 32 == 0 else 1
     width = model_width // members
-    block = (rows, width)
+    block = (rows // parts, width)
     return pl.pallas_call(
         project_kernel,
-        out_shape=jax.ShapeDtypeStruct((rows, model_width), jnp.bfloat16),
+        out_shape=[
+            jax.ShapeDtypeStruct((rows, model_width), jnp.bfloat16),
+            jax.ShapeDtypeStruct(own_total.shape, jnp.int32),
+        ],
         in_specs=[
             pl.BlockSpec(memory_space=pltpu.VMEM),
             pl.BlockSpec(memory_space=pl.ANY),
+            pl.BlockSpec(memory_space=pltpu.VMEM),
         ],
-        out_specs=pl.BlockSpec(memory_space=pltpu.VMEM),
+        out_specs=[pl.BlockSpec(memory_space=pltpu.VMEM)] * 2,
         scratch_shapes=[
             pltpu.VMEM((members, inner, width), jnp.bfloat16),
-            pltpu.VMEM((fars, *block), jnp.bfloat16),
-            pltpu.VMEM((fars, *block), jnp.bfloat16),
-            pltpu.VMEM((fars - 1, *block), jnp.bfloat16),
-            pltpu.VMEM((fars - 1, *block), jnp.bfloat16),
-            pltpu.VMEM(block, jnp.float32),
+            pltpu.VMEM((parts * fars, *block), jnp.bfloat16),
+            pltpu.VMEM((parts * fars, *block), jnp.bfloat16),
+            pltpu.VMEM((parts * (fars - 1), *block), jnp.bfloat16),
+            pltpu.VMEM((parts * (fars - 1), *block), jnp.bfloat16),
+            pltpu.VMEM((parts, *block), jnp.float32),
+            pltpu.VMEM((groups - 1, *own_total.shape), jnp.int32),
             pltpu.SemaphoreType.DMA((members,)),
-            pltpu.SemaphoreType.DMA((2, fars)),
-            pltpu.SemaphoreType.DMA((2, fars - 1)),
-            pltpu.SemaphoreType.DMA((2, fars)),
-            pltpu.SemaphoreType.DMA((2, fars - 1)),
+            pltpu.SemaphoreType.DMA((2, parts * fars)),
+            pltpu.SemaphoreType.DMA((2, parts * (fars - 1))),
+            pltpu.SemaphoreType.DMA((2, parts * fars)),
+            pltpu.SemaphoreType.DMA((2, parts * (fars - 1))),
+            pltpu.SemaphoreType.DMA((2, groups - 1)),
         ],
         compiler_params=pltpu.CompilerParams(
             collective_id=0, has_side_effects=True, vmem_limit_bytes=40 * 1024 * 1024
         ),
-    )(normalized, out_weight)
+    )(normalized, out_weight, own_total)
 
 
 def local(
@@ -224,16 +269,14 @@
     head_dim = inner_dev // head_count
     tap_count = value_kernel.shape[0]
     kept_count = accepted * live_flags
-    accepted_total = total_over_dp(jnp.sum(kept_count).reshape(1))
-    flat_rows = tokens.reshape(row_total, model_width).astype(jnp.float32)
+    wide = tokens.astype(jnp.float32)
     normed = (
-        flat_rows
-        * lax.rsqrt(jnp.mean(flat_rows * flat_rows, axis=1, keepdims=True) + EPSILON)
-        * norm_gain
-    ).astype(jnp.bfloat16)
+        (wide * lax.rsqrt(jnp.mean(wide * wide, axis=2, keepdims=True) + EPSILON) * norm_gain)
+        .astype(jnp.bfloat16)
+        .reshape(row_total, model_width)
+    )
     parity = lax.axis_index("tensor") % 2
-    in_flat = in_weight.reshape(in_weight.shape[0], 2 * inner_dev)
-    inner_sum = jnp.dot(normed, in_flat, preferred_element_type=jnp.float32)
+    inner_sum = jnp.einsum("rd,dgi->rgi", normed, in_weight, preferred_element_type=jnp.float32)
     group_sum = jnp.dot(normed, group_weight, preferred_element_type=jnp.float32)
     step_raw = jnp.dot(normed, step_weight, preferred_element_type=jnp.float32)
     inner_proj = inner_sum.astype(jnp.bfloat16).reshape(requests, positions, 2 * inner_dev)
@@ -283,19 +326,23 @@
         jnp.exp(prefix_kept)[:, :, None, None] * initial
         + jnp.einsum("rjhp,rjn->rhpn", narrow(weighted), narrow(input_map), preferred_element_type=jnp.float32)
     ).astype(jnp.bfloat16)
-    gated = head_out.reshape(row_total, inner_dev) * jax.nn.silu(
-        gate_part.reshape(row_total, inner_dev).astype(jnp.float32)
-    )
-    own_squares = jnp.sum(gated * gated, axis=1)
+    gated = head_out.reshape(requests, positions, inner_dev) * jax.nn.silu(
+        gate_part.astype(jnp.float32)
+    )
+    own_squares = jnp.sum(gated * gated, axis=2)
     other_squares = swapped(own_squares, "tensor", 0)
     scale_rows = lax.rsqrt((own_squares + other_squares) / (2 * inner_dev) + EPSILON)
     valid_rows = (jnp.arange(positions)[None, :] < draft_lengths[:, None]) & (
         live_flags[:, None] == 1
     )
-    normalized = jnp.where(
-        valid_rows.reshape(row_total, 1), gated * scale_rows[:, None] * out_gain, 0.0
-    ).astype(jnp.bfloat16)
-    layer_rows = project(normalized, out_weight)
+    normalized = (
+        jnp.where(valid_rows[:, :, None], gated * scale_rows[:, :, None] * out_gain, 0.0)
+        .astype(jnp.bfloat16)
+        .reshape(row_total, inner_dev)
+    )
+    own_total = jnp.broadcast_to(jnp.sum(kept_count), (8, 128))
+    layer_rows, totals = project(normalized, out_weight, own_total)
+    accepted_total = totals[0, :1]
     value_kept = keep_window(value_seq, kept_count, tap_count - 1)
     group_kept = keep_window(group_seq, kept_count, tap_count - 1)
     return (

time: 121 us -> 93 us (0.77)
  the two profiles are of different devices: /device:TPU:22 before, /device:TPU:0 now
where the time goes in v2:
time: 93 us; the launch traced here: 92.5 us
  Pallas kernels  51.1 us (55%)
  matrix products  19.9 us (21%)
  other arithmetic  9.74 us (10%)
  local copies, waits for them, and re-layouts  7.55 us (8%)
  starting transfers between devices  3.14 us (3%)
  between operations  1.06 us (1%)
    pallas_call x1, Pallas kernels, project(): pl.pallas_call(project_kernel, out_shape=[jax.ShapeDtypeStruct((rows, mod...  51.1 us
    dot_general x1, matrix products, local(): jnp.einsum('rjhp,rjn->rhpn', narrow(weighted), narrow(input_map), preferr...  5.44 us
    dot_general x1, matrix products, local(): jnp.einsum('rd,dgi->rgi', normed, in_weight, preferred_element_type=jnp.f...  5.24 us
    dot_general x1, matrix products, local(): jnp.einsum('rhpn,rsn->rshp', scan_state, narrow(output_map), preferred_el...  4.42 us
    unnamed x46, local copies, waits for them, and re-layouts  3.61 us
    ppermute x2, starting transfers between devices, swapped(): return lax.ppermute(value, axis, pairs)  3.14 us
    dot_general x1, matrix products, local(): jnp.dot(normed, group_weight, preferred_element_type=jnp.float32)  2.08 us
    dot_general x1, matrix products, local(): step_raw = jnp.dot(normed, step_weight, preferred_element_type=jnp.float32)  2.06 us
  transfers between devices with their start and end apart: 2, of which 0 were waited for; matrix products, arithmetic and copies ran while one was open for 23% of the time, Pallas kernels for 0%

profile of v2, /device:TPU:0, one launch (start us, length us, event | category | flops | bytes accessed | tf_op | source)
XLA Modules:
  0.0 92.5 jit_solution(3550883104792727496)
XLA Ops:
  0.7 0.8 convert_element_type.175
  1.5 0.8 bitcast_convert_fusion.3
  2.4 1.8 %fusion.2 = f32[24,8]{1,0:T(8,128)S(1)} fusion(bf16[24,8,4096]{2,1,0:T(8,128)(2,1)} %param.20), kind=kLoop, calls=%fused_computation.5 | loop fusion | flops 2359104 | bytes 1573632 | tf_op jit(solution)/shard_map/reduce_sum | solution.py:274
  4.2 0.7 constant_dynamic-update-slice_fusion.1
  4.9 2.1 %fusion.18 = bf16[24,8,128]{2,1,0:T(8,128)(2,1)S(1)} fusion(bf16[4096,128]{1,0:T(8,128)(2,1)S(1)} %copy-done, bf16[24,8,4096]{2,1,0:T(8,128)(2,1)} %param.20, f32[4096]{0:T(1024)} %param.21, f32[24,8]{1,0:T(8,128)S(1)} %add_rsqrt_fusion.1), kind=kOutput, calls=%fused_computation.18 | convolution fusion | flops 204496896 | bytes 2687744 | tf_op jit(solution)/shard_map/dot_general | solution.py:280
  7.1 3.1 %collective-permute-start = (bf16[24,8,128]{2,0,1:T(8,128)(2,1)S(1)}, bf16[24,8,128]{2,0,1:T(8,128)(2,1)}, u32[]{:S(2)}, u32[]{:S(2)}) collective-permute-start(bf16[24,8,128]{2,0,1:T(8,128)(2,1)S(1)} %divide_multiply_fusion.1), channel_id=1, source_target_pairs={{0,1},{1,0},{2,3},{3,2},{4,5},{5,4},{6,7},{7,6},{8,9},{9,8},{10,11... | collective-permute-start | bytes 147464 | tf_op jit(solution)/shard_map/ppermute | solution.py:18
  10.9 5.2 %fusion.10 = bf16[192,2,512]{2,0,1:T(8,128)(2,1)S(1)} fusion(bf16[4096,2,512]{2,1,0:T(2,128)(2,1)} %param.22, bf16[24,8,4096]{2,1,0:T(8,128)(2,1)S(1)} %copy-done.2, f32[4096]{0:T(1024)S(1)} %copy-done.16, f32[24,8]{1,0:T(8,128)S(1)} %add_rsqrt_fusion.1), kind=kOutput, calls=%fused_computation.15 | convolution fusion | flops 1613955072 | bytes 10371840 | tf_op jit(solution)/shard_map/rd,dgi->rgi/dot_general | solution.py:279
  16.9 0.7 fusion.64
  17.6 0.6 fusion.47
  18.7 0.7 fusion.65
  19.4 2.1 %negate_multiply_fusion = (f32[24,8,8]{2,1,0:T(8,128)S(1)}, f32[24,8,8]{2,1,0:T(8,128)S(1)}) fusion(f32[8]{0:T(128)S(1)} %copy-done.17, f32[8]{0:T(128)S(1)} %copy-done.18, bf16[4096,8]{0,1:T(8,128)(2,1)S(1)} %copy-done.15, bf16[24,8,4096]{2,1,0:T(8,128)(2,1)} %param.20, f32[4096]{0:T(1024)S(1)} %copy-done.16, f32[24,8]{1,0:T(8,128)S(1)} %add_rsqrt_fusion.1), kind=kOutput, calls=%fused_computation.67 | convolution fusion | flops 15742464 | bytes 1667904 | tf_op jit(solution)/shard_map/dot_general | solution.py:281
  21.8 0.5 copy-done.3
  22.6 0.6 iota_compare_fusion.3
  23.2 1.3 %reduce_sum.38 = s32[]{:T(128)} reduce(s32[24]{0:T(128)} %copy-done.9, s32[]{:T(128)} %constant.25.clone.1), dimensions={0}, to_apply=%region_3.4 | reduce | flops 23 | bytes 104 | tf_op jit(solution)/shard_map/reduce_sum | solution.py:343
  24.5 1.3 %exp.41 = f32[24,8]{1,0:T(8,128)} exponential(f32[24,8]{1,0:T(8,128)} %copy-done.3) | non-fusion elementwise | bytes 1536 | tf_op jit(solution)/shard_map/exp | solution.py:326
  26.1 0.7 copy.65
  26.8 0.8 select_convert_fusion.1
  27.7 4.4 %convolution_multiply_fusion = f32[24,8,8,64]{3,1,2,0:T(8,128)S(1)} fusion(bf16[24,8,64,128]{3,2,1,0:T(8,128)(2,1)} %param.34, f32[24,8,8]{1,2,0:T(8,128)S(1)} %copy.53, bf16[24,8,128]{2,0,1:T(8,128)(2,1)S(1)} %get-tuple-element.21), kind=kOutput, calls=%fused_computation.14 | convolution fusion | flops 25264128 | bytes 3594240 | tf_op jit(solution)/shard_map/rhpn,rsn->rshp/dot_general | solution.py:309
  32.2 0.5 fusion.9
  33.4 5.4 %add_convert_fusion = bf16[24,8,64,128]{3,2,1,0:T(8,128)(2,1)} fusion(bf16[24,8,64,128]{3,2,1,0:T(8,128)(2,1)} %param.34, f32[24,8]{1,0:T(8,128)S(1)} %copy-done.6, bf16[24,8,8,64]{3,2,1,0:T(8,128)(2,1)S(1)} %get-tuple-element.16, bf16[24,8,128]{2,0,1:T(8,128)(2,1)S(1)} %get-tuple-element.20), kind=kOutput, calls=%fused_computation.2 | convolution fusion | flops 31457280 | bytes 6537984 | tf_op jit(solution)/shard_map/rjhp,rjn->rhpn/dot_general | solution.py:327
  39.1 0.6 broadcast_in_dim.191.count_ref
  39.8 51.1 %shard_map.227 = (bf16[192,4096]{1,0:T(8,128)(2,1)S(1)}, s32[8,128]{1,0:T(8,128)S(1)}) custom-call(bf16[192,512]{1,0:T(8,128)(2,1)S(1)} %fusion.36.normalized_ref, bf16[512,4096]{1,0:T(8,128)(2,1)S(1)} %copy-done.1, s32[8,128]{1,0:T(8,128)S(1)} %broadcast_in_dim.191.count_ref), custom_call_target="tpu_custom_call" | custom-call | tf_op jit(solution)/shard_map/pallas_call | solution.py:210
  90.9 0.5 slice.137
  91.4 1.1 %copy.96 = bf16[24,8,4096]{2,1,0:T(8,128)(2,1)} copy(bf16[24,8,4096]{2,1,0:T(8,128)(2,1)S(1)} %bitcast.60) | data formatting | bytes 3145728
  (72 shorter events, 4.0 us)
Async XLA Ops:
  0.6 4.3 %copy-start = (bf16[4096,128]{1,0:T(8,128)(2,1)S(1)}, bf16[4096,128]{1,0:T(8,128)(2,1)}, u32[]{:S(2)}) copy-start(bf16[4096,128]{1,0:T(8,128)(2,1)} %param.23) | copy-start | bytes 3145732
  0.6 10.2 %copy-start.2 = (bf16[24,8,4096]{2,1,0:T(8,128)(2,1)S(1)}, bf16[24,8,4096]{2,1,0:T(8,128)(2,1)}, u32[]{:S(2)}) copy-start(bf16[24,8,4096]{2,1,0:T(8,128)(2,1)} %param.20) | copy-start | bytes 4718596
  0.7 10.2 %copy-start.16 = (f32[4096]{0:T(1024)S(1)}, f32[4096]{0:T(1024)}, u32[]{:S(2)}) copy-start(f32[4096]{0:T(1024)} %param.21) | copy-start | bytes 49156
  0.7 9.5 %copy-start.13 = (s32[24]{0:T(128)S(1)}, s32[24]{0:T(128)}, u32[]{:S(2)}) copy-start(s32[24]{0:T(128)} %param.39) | copy-start | bytes 292
  0.7 9.5 %copy-start.12 = (s32[24]{0:T(128)S(1)}, s32[24]{0:T(128)}, u32[]{:S(2)}) copy-start(s32[24]{0:T(128)} %param.37) | copy-start | bytes 292
  0.7 10.1 %copy-start.11 = (bf16[512]{0:T(512)(128)(2,1)S(1)}, bf16[512]{0:T(512)(128)(2,1)}, u32[]{:S(2)}) copy-start(bf16[512]{0:T(512)(128)(2,1)} %param.26) | copy-start | bytes 3076
  0.7 10.1 %copy-start.7 = (bf16[4,512]{1,0:T(4,128)(2,1)S(1)}, bf16[4,512]{1,0:T(4,128)(2,1)}, u32[]{:S(2)}) copy-start(bf16[4,512]{1,0:T(4,128)(2,1)} %param.25) | copy-start | bytes 12292
  0.7 10.1 %copy-start.5 = (bf16[24,3,512]{2,0,1:T(8,128)(2,1)S(1)}, bf16[24,3,512]{2,0,1:T(8,128)(2,1)}, u32[]{:S(2)}) copy-start(bf16[24,3,512]{2,0,1:T(8,128)(2,1)} %param.35) | copy-start | bytes 221188
  7.1 19.7 %collective-permute-start = (bf16[24,8,128]{2,0,1:T(8,128)(2,1)S(1)}, bf16[24,8,128]{2,0,1:T(8,128)(2,1)}, u32[]{:S(2)}, u32[]{:S(2)}) collective-permute-start(bf16[24,8,128]{2,0,1:T(8,128)(2,1)S(1)} %divide_multiply_fusion.1), channel_id=1, source_target_pairs={{0,1},{1,0},{2,3},{3,2},{4,5},{5,4},{6,7},{7,6},{8,9},{9,8},{10,11... | collective-permute-start | bytes 147464 | tf_op jit(solution)/shard_map/ppermute | solution.py:18
  10.2 0.5 copy-start.9
  10.9 6.0 %copy-start.4 = (bf16[24,3,128]{2,0,1:T(8,128)(2,1)S(1)}, bf16[24,3,128]{2,0,1:T(8,128)(2,1)}, u32[]{:S(2)}) copy-start(bf16[24,3,128]{2,0,1:T(8,128)(2,1)} %param.36) | copy-start | bytes 55300
  16.1 2.6 %copy-start.14 = (s32[24]{0:T(128)S(1)}, s32[24]{0:T(128)}, u32[]{:S(2)}) copy-start(s32[24]{0:T(128)} %param.38) | copy-start | bytes 292
  16.1 3.3 %copy-start.15 = (bf16[4096,8]{0,1:T(8,128)(2,1)S(1)}, bf16[4096,8]{0,1:T(8,128)(2,1)}, u32[]{:S(2)}) copy-start(bf16[4096,8]{0,1:T(8,128)(2,1)} %param.24) | copy-start | bytes 196612
  16.1 3.3 %copy-start.17 = (f32[8]{0:T(128)S(1)}, f32[8]{0:T(128)}, u32[]{:S(2)}) copy-start(f32[8]{0:T(128)} %param.30) | copy-start | bytes 100
  16.2 3.2 %copy-start.18 = (f32[8]{0:T(128)S(1)}, f32[8]{0:T(128)}, u32[]{:S(2)}) copy-start(f32[8]{0:T(128)} %param.29) | copy-start | bytes 100
  21.7 0.6 copy-start.3
  26.1 6.1 %copy-start.19 = (f32[8]{0:T(128)S(1)}, f32[8]{0:T(128)}, u32[]{:S(2)}) copy-start(f32[8]{0:T(128)} %param.31) | copy-start | bytes 100
  26.1 6.0 %copy-start.20 = (pred[8,8]{1,0:T(8,128)(4,1)S(1)}, pred[8,8]{1,0:T(8,128)(4,1)}, u32[]{:S(2)}) copy-start(pred[8,8]{1,0:T(8,128)(4,1)} %iota_compare_fusion.3) | copy-start | bytes 196
  32.2 1.2 %copy-start.6 = (f32[24,8]{1,0:T(8,128)S(1)}, f32[24,8]{1,0:T(8,128)}, u32[]{:S(2)}) copy-start(f32[24,8]{1,0:T(8,128)} %exp.41) | copy-start | bytes 2308
  33.3 5.6 %collective-permute-start.1 = (f32[24,8]{1,0:T(8,128)S(1)}, f32[24,8]{1,0:T(8,128)S(1)}, u32[]{:S(2)}, u32[]{:S(2)}) collective-permute-start(f32[24,8]{1,0:T(8,128)S(1)} %multiply_reduce_fusion), channel_id=1, source_target_pairs={{0,1},{1,0},{2,3},{3,2},{4,5},{5,4},{6,7},{7,6},{8,9},{9,8},{10,11... | collective-permute-start | bytes 2312 | tf_op jit(solution)/shard_map/ppermute | solution.py:18
  33.4 5.5 %copy-start.8 = (pred[24,8]{1,0:T(8,128)(4,1)S(1)}, pred[24,8]{1,0:T(8,128)(4,1)}, u32[]{:S(2)}) copy-start(pred[24,8]{1,0:T(8,128)(4,1)} %fusion.65) | copy-start | bytes 580
  33.4 5.5 %copy-start.10 = (f32[512]{0:T(512)S(1)}, f32[512]{0:T(512)}, u32[]{:S(2)}) copy-start(f32[512]{0:T(512)} %param.32) | copy-start | bytes 6148
  33.4 6.3 %copy-start.1 = (bf16[512,4096]{1,0:T(8,128)(2,1)S(1)}, bf16[512,4096]{1,0:T(8,128)(2,1)}, u32[]{:S(2)}) copy-start(bf16[512,4096]{1,0:T(8,128)(2,1)} %weight_ref.1) | copy-start | bytes 12582916
